TPU v7x, 32 devices: a whole 2x2x4 slice. The times are simulated.
32 devices in a mesh: gx: 4 (over y, x), gy: 2 (over core), gz: 4 (over z).
Axes of the slice: x: 2, y: 2, z: 4, core: 2. Of those that a mesh axis runs over, the one named last changes fastest.
Arguments:
- gradient: float32 [4, 2, 4, 16, 512], P('gx', 'gy', 'gz'), may hold values from -60 to 60
- local_schur: bfloat16 [4, 2, 4, 2048, 2048], P('gx', 'gy', 'gz'), may hold values from -1 to 4
- inverse_rows: bfloat16 [4, 2, 4, 512, 2048], P('gx', 'gy', 'gz'), may hold values from -0.1 to 0.6
- face_maps: int32 [4, 2, 4, 6, 256], P('gx', 'gy', 'gz'), may hold values from 0 to 511, as said below
Outputs:
- adjoint: float32 [4, 2, 4, 16, 512], P('gx', 'gy', 'gz')
- residual_ratio: float32 [16], replicated
Inputs may be any that keep to these rules, and one draw needn't show every extreme that they name: `face_maps`: for each subdomain and face, 256 distinct owned rows of the neighbour across that face.
All inputs are finite; a program needn't handle non-finite values.
Results may differ from a plain program's by a relative error of at most 0.0038.
Values may be sent and summed in bfloat16 or wider, within the bound.
A program may use at most 64 MiB of HBM per device.

v0:
```python
import jax
import jax.numpy as jnp
from jax import lax
from jax.sharding import PartitionSpec as P

ITERS = 3


EPSILON = 1e-06
FACE_SPOTS = ((0, 1, 1), (2, 1, 1), (1, 0, 1), (1, 2, 1), (1, 1, 0), (1, 1, 2))


def from_behind(array, axis, by):
    devices = lax.axis_size(axis)
    pairs = [(i, i + by) for i in range(devices) if 0 <= i + by < devices]
    return lax.ppermute(array, axis, pairs)


def with_halo(block, sides, width):
    for axis, dim in sides:
        count = lax.axis_size(axis)
        forward = [(i, i + 1) for i in range(count - 1)]
        backward = [(target, source) for source, target in forward]
        low = lax.ppermute(
            lax.slice_in_dim(block, block.shape[dim] - width, None, axis=dim), axis, forward
        )
        high = lax.ppermute(lax.slice_in_dim(block, 0, width, axis=dim), axis, backward)
        block = jnp.concatenate([low, block, high], axis=dim)
    return block


def pass_sums(outgoing):
    incoming = [None] * 6
    for offset, source_face, target_face in ((-1, 0, 1), (1, 1, 0)):
        incoming[target_face] = from_behind(outgoing[source_face], "gx", offset)
        incoming[target_face + 2] = from_behind(outgoing[source_face + 2], "gy", offset)
        incoming[target_face + 4] = from_behind(outgoing[source_face + 4], "gz", offset)
    return incoming


def gather_local(rounded, owned_maps):
    ghost_layer = with_halo(rounded[None, None, None], (("gx", 0), ("gy", 1), ("gz", 2)), 1)
    ghosts = [
        jnp.take(ghost_layer[FACE_SPOTS[facing]], owned_maps[facing], axis=1) for facing in range(6)
    ]
    return jnp.concatenate([rounded] + ghosts, axis=1)


def assemble(products, owned_maps):
    face_width = owned_maps.shape[1]
    owned = products.shape[1] - 6 * face_width
    result = products[:, :owned]
    face_blocks = [
        products[:, owned + facing * face_width : owned + (facing + 1) * face_width]
        for facing in range(6)
    ]
    outgoing = [
        jnp.zeros_like(result).at[:, owned_maps[facing]].add(face_blocks[facing])
        for facing in range(6)
    ]
    incoming = pass_sums(outgoing)
    for facing in range(6):
        result = result + incoming[facing]
    return result


def inner_local(left_side, right_side):
    return jnp.sum(left_side * right_side, axis=1)


def rotate_solve(columns, beta_norm):
    num_cols = len(columns)
    rhs_vec = [beta_norm] + [jnp.zeros_like(beta_norm) for unused in range(num_cols)]
    cosines = []
    sines = []
    triangle = []
    for section in range(num_cols):
        column = [columns[section][row_at] for row_at in range(section + 2)]
        for earlier in range(section):
            rotated_a = cosines[earlier] * column[earlier] + sines[earlier] * column[earlier + 1]
            rotated_b = -sines[earlier] * column[earlier] + cosines[earlier] * column[earlier + 1]
            column[earlier] = rotated_a
            column[earlier + 1] = rotated_b
        radius = jnp.sqrt(
            column[section] * column[section] + column[section + 1] * column[section + 1]
        )
        cosine = column[section] / radius
        sine_val = column[section + 1] / radius
        column[section] = radius
        cosines.append(cosine)
        sines.append(sine_val)
        rhs_vec[section + 1] = -sine_val * rhs_vec[section]
        rhs_vec[section] = cosine * rhs_vec[section]
        triangle.append(column[: section + 1])
    coeffs = [None] * num_cols
    for section in reversed(range(num_cols)):
        running = rhs_vec[section]
        for onward in range(section + 1, num_cols):
            running = running - triangle[onward][section] * coeffs[onward]
        coeffs[section] = running / triangle[section][section]
    return (coeffs, jnp.abs(rhs_vec[num_cols]))


def local(gradient, local_schur, inverse_rows, face_maps):
    target = gradient[0, 0, 0]
    schur_block = local_schur[0, 0, 0]
    restricted = inverse_rows[0, 0, 0]
    owned_maps = face_maps[0, 0, 0]
    initial = lax.psum(inner_local(target, target), ("gx", "gy", "gz"))
    beta_norm = jnp.sqrt(initial + EPSILON)
    krylov = [target / beta_norm[:, None]]
    directions = []
    columns = []
    gram_rows = []
    for section in range(ITERS):
        rounded = krylov[section].astype(jnp.bfloat16)
        prepared = assemble(
            jnp.dot(rounded, restricted, preferred_element_type=jnp.float32), owned_maps
        )
        directions.append(prepared)
        transposed_rounded = prepared.astype(jnp.bfloat16)
        intersected = gather_local(transposed_rounded, owned_maps)
        applied = assemble(
            jnp.dot(intersected, schur_block, preferred_element_type=jnp.float32), owned_maps
        )
        local_coeffs = jnp.stack([inner_local(vector, applied) for vector in krylov])
        local_gram = jnp.stack([inner_local(krylov[section], vector) for vector in krylov])
        coeffs, squares, gram_row = lax.psum(
            (local_coeffs, inner_local(applied, applied), local_gram), ("gx", "gy", "gz")
        )
        gram_rows.append(gram_row)
        residue = applied
        for position in range(section + 1):
            residue = residue - coeffs[position][:, None] * krylov[position]
        running = squares
        for earlier in range(section + 1):
            running = running - 2.0 * coeffs[earlier] * coeffs[earlier]
            for onward in range(section + 1):
                element = gram_rows[max(earlier, onward)][min(earlier, onward)]
                running = running + coeffs[earlier] * element * coeffs[onward]
        height = jnp.sqrt(jnp.maximum(running, 0.0) + EPSILON)
        columns.append([coeffs[position] for position in range(section + 1)] + [height])
        if section + 1 < ITERS:
            krylov.append(residue / height[:, None])
    weights, remainder = rotate_solve(columns, beta_norm)
    adjoint = weights[0][:, None] * directions[0]
    for position in range(1, ITERS):
        adjoint = adjoint + weights[position][:, None] * directions[position]
    return (adjoint[None, None, None], remainder / beta_norm)


def solution(mesh):
    placed = (
        P("gx", "gy", "gz", None, None),
        P("gx", "gy", "gz", None, None),
        P("gx", "gy", "gz", None, None),
        P("gx", "gy", "gz", None, None),
    )
    return jax.shard_map(
        local,
        mesh=mesh,
        in_specs=placed,
        out_specs=(P("gx", "gy", "gz", None, None), P()),
        check_vma=False,
    )
```

profile of v0, /device:TPU:0, one launch (start us, length us, event | category | flops | bytes accessed | tf_op | source)
XLA Modules:
  0.0 447.1 jit_solution(11915345555670398108)
XLA Ops:
  1.7 42.0 %psum.70 = f32[16]{0:T(128)S(1)} all-reduce(f32[16]{0:T(128)S(1)} %fusion.114), channel_id=1, replica_groups=mesh['gx'=4,'gy'=2,'gz'=4] {'gx','gy','gz'}, use_global_device_ids=true, to_apply=%region_1.0 | all-reduce | flops 16 | bytes 128 | tf_op jit(solution)/shard_map/psum | solution.py:109
  45.8 1.5 scatter_custom_fusion
  47.3 4.2 collective-permute-start
  51.6 1.5 scatter_custom_fusion.5
  56.2 4.5 %collective-permute-start.4 = (f32[16,512]{1,0:T(8,128)S(1)}, f32[16,512]{1,0:T(8,128)S(1)}, u32[]{:S(2)}, u32[]{:S(2)}) collective-permute-start(f32[16,512]{1,0:T(8,128)S(1)} %copy.123), channel_id=1, source_target_pairs={{0,1},{1,2},{2,3},{4,5},{5,6},{6,7},{8,9},{9,10},{10,11},{12,13},{... | collective-permute-start | bytes 98312 | tf_op jit(solution)/shard_map/ppermute | solution.py:16
  65.4 3.0 collective-permute-start.2
  69.6 1.5 scatter_custom_fusion.1
  72.5 4.5 collective-permute-done.1
  78.3 4.9 %collective-permute-start.6 = (bf16[1,1,1,16,512]{4,3,2,1,0:T(8,128)(2,1)S(1)}, bf16[1,1,1,16,512]{4,3,2,1,0:T(8,128)(2,1)S(1)}, u32[]{:S(2)}, u32[]{:S(2)}) collective-permute-start(bf16[1,1,1,16,512]{4,3,2,1,0:T(8,128)(2,1)S(1)} %get-tuple-element.44), channel_id=1, source_target_pairs={{0,8},{8,16},{16,24},{1,9},{9,17},{17,25},{2,10},{10,18},{18,26},{... | collective-permute-start | bytes 49160 | tf_op jit(solution)/shard_map/ppermute | solution.py:24
  85.9 3.0 collective-permute-start.8
  92.5 5.0 %collective-permute-start.10 = (bf16[3,3,1,16,512]{4,3,2,1,0:T(8,128)(2,1)S(1)}, bf16[3,3,1,16,512]{4,3,2,1,0:T(8,128)(2,1)S(1)}, u32[]{:S(2)}, u32[]{:S(2)}) collective-permute-start(bf16[3,3,1,16,512]{4,3,2,1,0:T(8,128)(2,1)S(1)} %pad_maximum_fusion), channel_id=1, source_target_pairs={{0,1},{1,2},{2,3},{4,5},{5,6},{6,7},{8,9},{9,10},{10,11},{12,13},{... | collective-permute-start | bytes 442376 | tf_op jit(solution)/shard_map/ppermute | solution.py:24
  101.9 4.6 %fusion.4 = f32[16,2048]{1,0:T(8,128)S(1)} fusion(bf16[16,2048]{1,0:T(8,128)(2,1)S(1)} %constant_dynamic-update-slice_fusion, bf16[1,1,1,2048,2048]{4,3,2,1,0:T(8,128)(2,1)} %param.7), kind=kOutput, calls=%fused_computation.58 | convolution fusion | flops 134217728 | bytes 8585216 | tf_op jit(solution)/shard_map/dot_general | solution.py:124
  108.1 4.8 %collective-permute-start.12 = (f32[16,512]{1,0:T(8,128)S(1)}, f32[16,512]{1,0:T(8,128)S(1)}, u32[]{:S(2)}, u32[]{:S(2)}) collective-permute-start(f32[16,512]{1,0:T(8,128)S(1)} %copy.139), channel_id=1, source_target_pairs={{0,8},{8,16},{16,24},{1,9},{9,17},{17,25},{2,10},{10,18},{18,26},{... | collective-permute-start | bytes 98312 | tf_op jit(solution)/shard_map/ppermute | solution.py:16
  117.7 4.5 %collective-permute-start.16 = (f32[16,512]{1,0:T(8,128)S(1)}, f32[16,512]{1,0:T(8,128)S(1)}, u32[]{:S(2)}, u32[]{:S(2)}) collective-permute-start(f32[16,512]{1,0:T(8,128)S(1)} %copy.147), channel_id=1, source_target_pairs={{0,1},{1,2},{2,3},{4,5},{5,6},{6,7},{8,9},{9,10},{10,11},{12,13},{... | collective-permute-start | bytes 98312 | tf_op jit(solution)/shard_map/ppermute | solution.py:16
  126.9 3.0 collective-permute-start.14
  133.0 5.7 %collective-permute-done.13 = f32[16,512]{1,0:T(8,128)S(1)} collective-permute-done((f32[16,512]{1,0:T(8,128)S(1)}, f32[16,512]{1,0:T(8,128)S(1)}, u32[]{:S(2)}, u32[]{:S(2)}) %collective-permute-start.13) | collective-permute-done | bytes 32800 | tf_op jit(solution)/shard_map/ppermute | solution.py:16
  138.8 40.2 %all-reduce.2 = (f32[16]{0:T(128)S(1)}, f32[16]{0:T(128)S(1)}, f32[16]{0:T(128)S(1)}) all-reduce(f32[16]{0:T(128)S(1)} %get-tuple-element.10, f32[16]{0:T(128)S(1)} %get-tuple-element.9, f32[16]{0:T(128)S(1)} %get-tuple-element.11), channel_id=1, replica_groups=mesh['gx'=4,'gy'=2,'gz'=4] {'gx','gy','gz'}, use_global_device_ids=true, to_apply=%region_15.17 | all-reduce | flops 48 | bytes 384 | tf_op jit(solution)/shard_map/psum | solution.py:128
  179.7 1.5 scatter_custom_fusion.12
  181.3 4.4 collective-permute-start.18
  190.3 4.5 %collective-permute-start.22 = (f32[16,512]{1,0:T(8,128)S(1)}, f32[16,512]{1,0:T(8,128)S(1)}, u32[]{:S(2)}, u32[]{:S(2)}) collective-permute-start(f32[16,512]{1,0:T(8,128)S(1)} %copy.159), channel_id=1, source_target_pairs={{0,1},{1,2},{2,3},{4,5},{5,6},{6,7},{8,9},{9,10},{10,11},{12,13},{... | collective-permute-start | bytes 98312 | tf_op jit(solution)/shard_map/ppermute | solution.py:16
  199.5 3.0 collective-permute-start.20
  205.6 4.5 collective-permute-done.19
  211.4 4.9 %collective-permute-start.24 = (bf16[1,1,1,16,512]{4,3,2,1,0:T(8,128)(2,1)S(1)}, bf16[1,1,1,16,512]{4,3,2,1,0:T(8,128)(2,1)S(1)}, u32[]{:S(2)}, u32[]{:S(2)}) collective-permute-start(bf16[1,1,1,16,512]{4,3,2,1,0:T(8,128)(2,1)S(1)} %get-tuple-element.41), channel_id=1, source_target_pairs={{0,8},{8,16},{16,24},{1,9},{9,17},{17,25},{2,10},{10,18},{18,26},{... | collective-permute-start | bytes 49160 | tf_op jit(solution)/shard_map/ppermute | solution.py:24
  219.0 3.0 collective-permute-start.26
  225.6 4.6 %collective-permute-start.28 = (bf16[3,3,1,16,512]{4,3,2,1,0:T(8,128)(2,1)S(1)}, bf16[3,3,1,16,512]{4,3,2,1,0:T(8,128)(2,1)S(1)}, u32[]{:S(2)}, u32[]{:S(2)}) collective-permute-start(bf16[3,3,1,16,512]{4,3,2,1,0:T(8,128)(2,1)S(1)} %pad_maximum_fusion.1), channel_id=1, source_target_pairs={{0,1},{1,2},{2,3},{4,5},{5,6},{6,7},{8,9},{9,10},{10,11},{12,13},{... | collective-permute-start | bytes 442376 | tf_op jit(solution)/shard_map/ppermute | solution.py:24
  234.5 4.6 %fusion.2 = f32[16,2048]{1,0:T(8,128)S(1)} fusion(bf16[16,2048]{1,0:T(8,128)(2,1)S(1)} %constant_dynamic-update-slice_fusion.7, bf16[1,1,1,2048,2048]{4,3,2,1,0:T(8,128)(2,1)} %param.7), kind=kOutput, calls=%fused_computation.56 | convolution fusion | flops 134217728 | bytes 8585216 | tf_op jit(solution)/shard_map/dot_general | solution.py:124
  240.8 4.8 %collective-permute-start.30 = (f32[16,512]{1,0:T(8,128)S(1)}, f32[16,512]{1,0:T(8,128)S(1)}, u32[]{:S(2)}, u32[]{:S(2)}) collective-permute-start(f32[16,512]{1,0:T(8,128)S(1)} %copy.175), channel_id=1, source_target_pairs={{0,8},{8,16},{16,24},{1,9},{9,17},{17,25},{2,10},{10,18},{18,26},{... | collective-permute-start | bytes 98312 | tf_op jit(solution)/shard_map/ppermute | solution.py:16
  247.3 1.5 collective-permute-start.35
  250.5 4.5 %collective-permute-start.34 = (f32[16,512]{1,0:T(8,128)S(1)}, f32[16,512]{1,0:T(8,128)S(1)}, u32[]{:S(2)}, u32[]{:S(2)}) collective-permute-start(f32[16,512]{1,0:T(8,128)S(1)} %copy.183), channel_id=1, source_target_pairs={{0,1},{1,2},{2,3},{4,5},{5,6},{6,7},{8,9},{9,10},{10,11},{12,13},{... | collective-permute-start | bytes 98312 | tf_op jit(solution)/shard_map/ppermute | solution.py:16
  255.1 1.5 scatter_custom_fusion.21
  259.7 3.0 collective-permute-start.32
  265.8 5.7 %collective-permute-done.31 = f32[16,512]{1,0:T(8,128)S(1)} collective-permute-done((f32[16,512]{1,0:T(8,128)S(1)}, f32[16,512]{1,0:T(8,128)S(1)}, u32[]{:S(2)}, u32[]{:S(2)}) %collective-permute-start.31) | collective-permute-done | bytes 32800 | tf_op jit(solution)/shard_map/ppermute | solution.py:16
  271.7 40.6 %all-reduce.1 = (f32[16]{0:T(128)S(1)}, f32[2,16]{1,0:T(2,128)S(1)}, f32[2,16]{1,0:T(2,128)S(1)}) all-reduce(f32[16]{0:T(128)S(1)} %get-tuple-element.17, f32[2,16]{1,0:T(2,128)S(1)} %get-tuple-element.97, f32[2,16]{1,0:T(2,128)S(1)} %get-tuple-element.96), channel_id=1, replica_groups=mesh['gx'=4,'gy'=2,'gz'=4] {'gx','gy','gz'}, use_global_device_ids=true, to_apply=%region_36.38 | all-reduce | flops 80 | bytes 640 | tf_op jit(solution)/shard_map/psum | solution.py:128
  312.9 1.5 scatter_custom_fusion.24
  314.5 4.2 collective-permute-start.36
  323.3 4.5 %collective-permute-start.40 = (f32[16,512]{1,0:T(8,128)S(1)}, f32[16,512]{1,0:T(8,128)S(1)}, u32[]{:S(2)}, u32[]{:S(2)}) collective-permute-start(f32[16,512]{1,0:T(8,128)S(1)} %copy.195), channel_id=1, source_target_pairs={{0,1},{1,2},{2,3},{4,5},{5,6},{6,7},{8,9},{9,10},{10,11},{12,13},{... | collective-permute-start | bytes 98312 | tf_op jit(solution)/shard_map/ppermute | solution.py:16
  332.6 3.0 collective-permute-start.38
  335.7 1.7 scatter_custom_fusion.25
  338.9 4.5 collective-permute-done.37
  344.7 4.9 %collective-permute-start.42 = (bf16[1,1,1,16,512]{4,3,2,1,0:T(8,128)(2,1)S(1)}, bf16[1,1,1,16,512]{4,3,2,1,0:T(8,128)(2,1)S(1)}, u32[]{:S(2)}, u32[]{:S(2)}) collective-permute-start(bf16[1,1,1,16,512]{4,3,2,1,0:T(8,128)(2,1)S(1)} %get-tuple-element.38), channel_id=1, source_target_pairs={{0,8},{8,16},{16,24},{1,9},{9,17},{17,25},{2,10},{10,18},{18,26},{... | collective-permute-start | bytes 49160 | tf_op jit(solution)/shard_map/ppermute | solution.py:24
  352.3 3.0 collective-permute-start.44
  358.8 4.6 %collective-permute-start.46 = (bf16[3,3,1,16,512]{4,3,2,1,0:T(8,128)(2,1)S(1)}, bf16[3,3,1,16,512]{4,3,2,1,0:T(8,128)(2,1)S(1)}, u32[]{:S(2)}, u32[]{:S(2)}) collective-permute-start(bf16[3,3,1,16,512]{4,3,2,1,0:T(8,128)(2,1)S(1)} %pad_maximum_fusion.2), channel_id=1, source_target_pairs={{0,1},{1,2},{2,3},{4,5},{5,6},{6,7},{8,9},{9,10},{10,11},{12,13},{... | collective-permute-start | bytes 442376 | tf_op jit(solution)/shard_map/ppermute | solution.py:24
  367.8 4.6 %fusion = f32[16,2048]{1,0:T(8,128)S(1)} fusion(bf16[16,2048]{1,0:T(8,128)(2,1)S(1)} %constant_dynamic-update-slice_fusion.14, bf16[1,1,1,2048,2048]{4,3,2,1,0:T(8,128)(2,1)} %param.7), kind=kOutput, calls=%fused_computation.54 | convolution fusion | flops 134217728 | bytes 8585216 | tf_op jit(solution)/shard_map/dot_general | solution.py:124
  374.1 4.8 %collective-permute-start.48 = (f32[16,512]{1,0:T(8,128)S(1)}, f32[16,512]{1,0:T(8,128)S(1)}, u32[]{:S(2)}, u32[]{:S(2)}) collective-permute-start(f32[16,512]{1,0:T(8,128)S(1)} %copy.211), channel_id=1, source_target_pairs={{0,8},{8,16},{16,24},{1,9},{9,17},{17,25},{2,10},{10,18},{18,26},{... | collective-permute-start | bytes 98312 | tf_op jit(solution)/shard_map/ppermute | solution.py:16
  383.6 4.5 %collective-permute-start.52 = (f32[16,512]{1,0:T(8,128)S(1)}, f32[16,512]{1,0:T(8,128)S(1)}, u32[]{:S(2)}, u32[]{:S(2)}) collective-permute-start(f32[16,512]{1,0:T(8,128)S(1)} %copy.219), channel_id=1, source_target_pairs={{0,1},{1,2},{2,3},{4,5},{5,6},{6,7},{8,9},{9,10},{10,11},{12,13},{... | collective-permute-start | bytes 98312 | tf_op jit(solution)/shard_map/ppermute | solution.py:16
  392.8 3.0 collective-permute-start.50
  398.9 5.7 %collective-permute-done.49 = f32[16,512]{1,0:T(8,128)S(1)} collective-permute-done((f32[16,512]{1,0:T(8,128)S(1)}, f32[16,512]{1,0:T(8,128)S(1)}, u32[]{:S(2)}, u32[]{:S(2)}) %collective-permute-start.49) | collective-permute-done | bytes 32800 | tf_op jit(solution)/shard_map/ppermute | solution.py:16
  404.8 40.6 %all-reduce = (f32[3,16]{1,0:T(4,128)S(1)}, f32[3,16]{1,0:T(4,128)S(1)}, f32[16]{0:T(128)S(1)}) all-reduce(f32[3,16]{1,0:T(4,128)S(1)} %pad_maximum_fusion.6, f32[3,16]{1,0:T(4,128)S(1)} %pad_maximum_fusion.7, f32[16]{0:T(128)S(1)} %get-tuple-element.13), channel_id=1, replica_groups=mesh['gx'=4,'gy'=2,'gz'=4] {'gx','gy','gz'}, use_global_device_ids=true, to_apply=%region_55.57 | all-reduce | flops 112 | bytes 896 | tf_op jit(solution)/shard_map/psum | solution.py:128
  (320 shorter events, 114.2 us)
Async XLA Ops:
  47.3 23.8 %collective-permute-start = (f32[16,512]{1,0:T(8,128)S(1)}, f32[16,512]{1,0:T(8,128)S(1)}, u32[]{:S(2)}, u32[]{:S(2)}) collective-permute-start(f32[16,512]{1,0:T(8,128)S(1)} %copy.115), channel_id=1, source_target_pairs={{0,8},{8,16},{16,24},{1,9},{9,17},{17,25},{2,10},{10,18},{18,26},{... | collective-permute-start | bytes 98312 | tf_op jit(solution)/shard_map/ppermute | solution.py:16
  53.2 19.3 %collective-permute-start.5 = (f32[16,512]{1,0:T(8,128)S(1)}, f32[16,512]{1,0:T(8,128)S(1)}, u32[]{:S(2)}, u32[]{:S(2)}) collective-permute-start(f32[16,512]{1,0:T(8,128)S(1)} %copy.125), channel_id=1, source_target_pairs={{1,0},{2,1},{3,2},{5,4},{6,5},{7,6},{9,8},{10,9},{11,10},{13,12},{... | collective-permute-start | bytes 98312 | tf_op jit(solution)/shard_map/ppermute | solution.py:16
  56.2 16.3 %collective-permute-start.4 = (f32[16,512]{1,0:T(8,128)S(1)}, f32[16,512]{1,0:T(8,128)S(1)}, u32[]{:S(2)}, u32[]{:S(2)}) collective-permute-start(f32[16,512]{1,0:T(8,128)S(1)} %copy.123), channel_id=1, source_target_pairs={{0,1},{1,2},{2,3},{4,5},{5,6},{6,7},{8,9},{9,10},{10,11},{12,13},{... | collective-permute-start | bytes 98312 | tf_op jit(solution)/shard_map/ppermute | solution.py:16
  62.5 10.0 %collective-permute-start.3 = (f32[16,512]{1,0:T(8,128)S(1)}, f32[16,512]{1,0:T(8,128)S(1)}, u32[]{:S(2)}, u32[]{:S(2)}) collective-permute-start(f32[16,512]{1,0:T(8,128)S(1)} %copy.121), channel_id=1, source_target_pairs={{4,0},{5,1},{6,2},{7,3},{12,8},{13,9},{14,10},{15,11},{20,16},{21,... | collective-permute-start | bytes 98312 | tf_op jit(solution)/shard_map/ppermute | solution.py:16
  65.4 7.1 %collective-permute-start.2 = (f32[16,512]{1,0:T(8,128)S(1)}, f32[16,512]{1,0:T(8,128)S(1)}, u32[]{:S(2)}, u32[]{:S(2)}) collective-permute-start(f32[16,512]{1,0:T(8,128)S(1)} %copy.119), channel_id=1, source_target_pairs={{0,4},{1,5},{2,6},{3,7},{8,12},{9,13},{10,14},{11,15},{16,20},{17,... | collective-permute-start | bytes 98312 | tf_op jit(solution)/shard_map/ppermute | solution.py:16
  77.0 6.2 %collective-permute-start.7 = (bf16[1,1,1,16,512]{4,3,2,1,0:T(8,128)(2,1)S(1)}, bf16[1,1,1,16,512]{4,3,2,1,0:T(8,128)(2,1)S(1)}, u32[]{:S(2)}, u32[]{:S(2)}) collective-permute-start(bf16[1,1,1,16,512]{4,3,2,1,0:T(8,128)(2,1)S(1)} %get-tuple-element.44), channel_id=1, source_target_pairs={{8,0},{16,8},{24,16},{9,1},{17,9},{25,17},{10,2},{18,10},{26,18},{... | collective-permute-start | bytes 49160 | tf_op jit(solution)/shard_map/ppermute | solution.py:27
  78.3 6.3 %collective-permute-start.6 = (bf16[1,1,1,16,512]{4,3,2,1,0:T(8,128)(2,1)S(1)}, bf16[1,1,1,16,512]{4,3,2,1,0:T(8,128)(2,1)S(1)}, u32[]{:S(2)}, u32[]{:S(2)}) collective-permute-start(bf16[1,1,1,16,512]{4,3,2,1,0:T(8,128)(2,1)S(1)} %get-tuple-element.44), channel_id=1, source_target_pairs={{0,8},{8,16},{16,24},{1,9},{9,17},{17,25},{2,10},{10,18},{18,26},{... | collective-permute-start | bytes 49160 | tf_op jit(solution)/shard_map/ppermute | solution.py:24
  84.6 6.5 %collective-permute-start.9 = (bf16[3,1,1,16,512]{4,3,2,1,0:T(8,128)(2,1)S(1)}, bf16[3,1,1,16,512]{4,3,2,1,0:T(8,128)(2,1)S(1)}, u32[]{:S(2)}, u32[]{:S(2)}) collective-permute-start(bf16[3,1,1,16,512]{4,3,2,1,0:T(8,128)(2,1)S(1)} %pad_maximum_fusion.3), channel_id=1, source_target_pairs={{4,0},{5,1},{6,2},{7,3},{12,8},{13,9},{14,10},{15,11},{20,16},{21,... | collective-permute-start | bytes 147464 | tf_op jit(solution)/shard_map/ppermute | solution.py:27
  91.2 8.5 %collective-permute-start.11 = (bf16[3,3,1,16,512]{4,3,2,1,0:T(8,128)(2,1)S(1)}, bf16[3,3,1,16,512]{4,3,2,1,0:T(8,128)(2,1)S(1)}, u32[]{:S(2)}, u32[]{:S(2)}) collective-permute-start(bf16[3,3,1,16,512]{4,3,2,1,0:T(8,128)(2,1)S(1)} %pad_maximum_fusion), channel_id=1, source_target_pairs={{1,0},{2,1},{3,2},{5,4},{6,5},{7,6},{9,8},{10,9},{11,10},{13,12},{... | collective-permute-start | bytes 442376 | tf_op jit(solution)/shard_map/ppermute | solution.py:27
  92.5 8.3 %collective-permute-start.10 = (bf16[3,3,1,16,512]{4,3,2,1,0:T(8,128)(2,1)S(1)}, bf16[3,3,1,16,512]{4,3,2,1,0:T(8,128)(2,1)S(1)}, u32[]{:S(2)}, u32[]{:S(2)}) collective-permute-start(bf16[3,3,1,16,512]{4,3,2,1,0:T(8,128)(2,1)S(1)} %pad_maximum_fusion), channel_id=1, source_target_pairs={{0,1},{1,2},{2,3},{4,5},{5,6},{6,7},{8,9},{9,10},{10,11},{12,13},{... | collective-permute-start | bytes 442376 | tf_op jit(solution)/shard_map/ppermute | solution.py:24
  108.1 23.5 %collective-permute-start.12 = (f32[16,512]{1,0:T(8,128)S(1)}, f32[16,512]{1,0:T(8,128)S(1)}, u32[]{:S(2)}, u32[]{:S(2)}) collective-permute-start(f32[16,512]{1,0:T(8,128)S(1)} %copy.139), channel_id=1, source_target_pairs={{0,8},{8,16},{16,24},{1,9},{9,17},{17,25},{2,10},{10,18},{18,26},{... | collective-permute-start | bytes 98312 | tf_op jit(solution)/shard_map/ppermute | solution.py:16
  114.7 18.3 %collective-permute-start.17 = (f32[16,512]{1,0:T(8,128)S(1)}, f32[16,512]{1,0:T(8,128)S(1)}, u32[]{:S(2)}, u32[]{:S(2)}) collective-permute-start(f32[16,512]{1,0:T(8,128)S(1)} %copy.149), channel_id=1, source_target_pairs={{1,0},{2,1},{3,2},{5,4},{6,5},{7,6},{9,8},{10,9},{11,10},{13,12},{... | collective-permute-start | bytes 98312 | tf_op jit(solution)/shard_map/ppermute | solution.py:16
  117.7 15.3 %collective-permute-start.16 = (f32[16,512]{1,0:T(8,128)S(1)}, f32[16,512]{1,0:T(8,128)S(1)}, u32[]{:S(2)}, u32[]{:S(2)}) collective-permute-start(f32[16,512]{1,0:T(8,128)S(1)} %copy.147), channel_id=1, source_target_pairs={{0,1},{1,2},{2,3},{4,5},{5,6},{6,7},{8,9},{9,10},{10,11},{12,13},{... | collective-permute-start | bytes 98312 | tf_op jit(solution)/shard_map/ppermute | solution.py:16
  123.9 9.0 %collective-permute-start.15 = (f32[16,512]{1,0:T(8,128)S(1)}, f32[16,512]{1,0:T(8,128)S(1)}, u32[]{:S(2)}, u32[]{:S(2)}) collective-permute-start(f32[16,512]{1,0:T(8,128)S(1)} %copy.145), channel_id=1, source_target_pairs={{4,0},{5,1},{6,2},{7,3},{12,8},{13,9},{14,10},{15,11},{20,16},{21,... | collective-permute-start | bytes 98312 | tf_op jit(solution)/shard_map/ppermute | solution.py:16
  126.9 6.1 %collective-permute-start.14 = (f32[16,512]{1,0:T(8,128)S(1)}, f32[16,512]{1,0:T(8,128)S(1)}, u32[]{:S(2)}, u32[]{:S(2)}) collective-permute-start(f32[16,512]{1,0:T(8,128)S(1)} %copy.143), channel_id=1, source_target_pairs={{0,4},{1,5},{2,6},{3,7},{8,12},{9,13},{10,14},{11,15},{16,20},{17,... | collective-permute-start | bytes 98312 | tf_op jit(solution)/shard_map/ppermute | solution.py:16
  131.6 7.0 %collective-permute-start.13 = (f32[16,512]{1,0:T(8,128)S(1)}, f32[16,512]{1,0:T(8,128)S(1)}, u32[]{:S(2)}, u32[]{:S(2)}) collective-permute-start(f32[16,512]{1,0:T(8,128)S(1)} %copy.141), channel_id=1, source_target_pairs={{8,0},{16,8},{24,16},{9,1},{17,9},{25,17},{10,2},{18,10},{26,18},{... | collective-permute-start | bytes 98312 | tf_op jit(solution)/shard_map/ppermute | solution.py:16
  181.3 23.0 %collective-permute-start.18 = (f32[16,512]{1,0:T(8,128)S(1)}, f32[16,512]{1,0:T(8,128)S(1)}, u32[]{:S(2)}, u32[]{:S(2)}) collective-permute-start(f32[16,512]{1,0:T(8,128)S(1)} %copy.151), channel_id=1, source_target_pairs={{0,8},{8,16},{16,24},{1,9},{9,17},{17,25},{2,10},{10,18},{18,26},{... | collective-permute-start | bytes 98312 | tf_op jit(solution)/shard_map/ppermute | solution.py:16
  187.3 18.3 %collective-permute-start.23 = (f32[16,512]{1,0:T(8,128)S(1)}, f32[16,512]{1,0:T(8,128)S(1)}, u32[]{:S(2)}, u32[]{:S(2)}) collective-permute-start(f32[16,512]{1,0:T(8,128)S(1)} %copy.161), channel_id=1, source_target_pairs={{1,0},{2,1},{3,2},{5,4},{6,5},{7,6},{9,8},{10,9},{11,10},{13,12},{... | collective-permute-start | bytes 98312 | tf_op jit(solution)/shard_map/ppermute | solution.py:16
  190.3 15.3 %collective-permute-start.22 = (f32[16,512]{1,0:T(8,128)S(1)}, f32[16,512]{1,0:T(8,128)S(1)}, u32[]{:S(2)}, u32[]{:S(2)}) collective-permute-start(f32[16,512]{1,0:T(8,128)S(1)} %copy.159), channel_id=1, source_target_pairs={{0,1},{1,2},{2,3},{4,5},{5,6},{6,7},{8,9},{9,10},{10,11},{12,13},{... | collective-permute-start | bytes 98312 | tf_op jit(solution)/shard_map/ppermute | solution.py:16
  196.5 9.0 %collective-permute-start.21 = (f32[16,512]{1,0:T(8,128)S(1)}, f32[16,512]{1,0:T(8,128)S(1)}, u32[]{:S(2)}, u32[]{:S(2)}) collective-permute-start(f32[16,512]{1,0:T(8,128)S(1)} %copy.157), channel_id=1, source_target_pairs={{4,0},{5,1},{6,2},{7,3},{12,8},{13,9},{14,10},{15,11},{20,16},{21,... | collective-permute-start | bytes 98312 | tf_op jit(solution)/shard_map/ppermute | solution.py:16
  199.5 6.1 %collective-permute-start.20 = (f32[16,512]{1,0:T(8,128)S(1)}, f32[16,512]{1,0:T(8,128)S(1)}, u32[]{:S(2)}, u32[]{:S(2)}) collective-permute-start(f32[16,512]{1,0:T(8,128)S(1)} %copy.155), channel_id=1, source_target_pairs={{0,4},{1,5},{2,6},{3,7},{8,12},{9,13},{10,14},{11,15},{16,20},{17,... | collective-permute-start | bytes 98312 | tf_op jit(solution)/shard_map/ppermute | solution.py:16
  210.1 6.2 %collective-permute-start.25 = (bf16[1,1,1,16,512]{4,3,2,1,0:T(8,128)(2,1)S(1)}, bf16[1,1,1,16,512]{4,3,2,1,0:T(8,128)(2,1)S(1)}, u32[]{:S(2)}, u32[]{:S(2)}) collective-permute-start(bf16[1,1,1,16,512]{4,3,2,1,0:T(8,128)(2,1)S(1)} %get-tuple-element.41), channel_id=1, source_target_pairs={{8,0},{16,8},{24,16},{9,1},{17,9},{25,17},{10,2},{18,10},{26,18},{... | collective-permute-start | bytes 49160 | tf_op jit(solution)/shard_map/ppermute | solution.py:27
  211.4 6.3 %collective-permute-start.24 = (bf16[1,1,1,16,512]{4,3,2,1,0:T(8,128)(2,1)S(1)}, bf16[1,1,1,16,512]{4,3,2,1,0:T(8,128)(2,1)S(1)}, u32[]{:S(2)}, u32[]{:S(2)}) collective-permute-start(bf16[1,1,1,16,512]{4,3,2,1,0:T(8,128)(2,1)S(1)} %get-tuple-element.41), channel_id=1, source_target_pairs={{0,8},{8,16},{16,24},{1,9},{9,17},{17,25},{2,10},{10,18},{18,26},{... | collective-permute-start | bytes 49160 | tf_op jit(solution)/shard_map/ppermute | solution.py:24
  217.7 6.5 %collective-permute-start.27 = (bf16[3,1,1,16,512]{4,3,2,1,0:T(8,128)(2,1)S(1)}, bf16[3,1,1,16,512]{4,3,2,1,0:T(8,128)(2,1)S(1)}, u32[]{:S(2)}, u32[]{:S(2)}) collective-permute-start(bf16[3,1,1,16,512]{4,3,2,1,0:T(8,128)(2,1)S(1)} %pad_maximum_fusion.4), channel_id=1, source_target_pairs={{4,0},{5,1},{6,2},{7,3},{12,8},{13,9},{14,10},{15,11},{20,16},{21,... | collective-permute-start | bytes 147464 | tf_op jit(solution)/shard_map/ppermute | solution.py:27
  224.3 8.0 %collective-permute-start.29 = (bf16[3,3,1,16,512]{4,3,2,1,0:T(8,128)(2,1)S(1)}, bf16[3,3,1,16,512]{4,3,2,1,0:T(8,128)(2,1)S(1)}, u32[]{:S(2)}, u32[]{:S(2)}) collective-permute-start(bf16[3,3,1,16,512]{4,3,2,1,0:T(8,128)(2,1)S(1)} %pad_maximum_fusion.1), channel_id=1, source_target_pairs={{1,0},{2,1},{3,2},{5,4},{6,5},{7,6},{9,8},{10,9},{11,10},{13,12},{... | collective-permute-start | bytes 442376 | tf_op jit(solution)/shard_map/ppermute | solution.py:27
  225.6 7.8 %collective-permute-start.28 = (bf16[3,3,1,16,512]{4,3,2,1,0:T(8,128)(2,1)S(1)}, bf16[3,3,1,16,512]{4,3,2,1,0:T(8,128)(2,1)S(1)}, u32[]{:S(2)}, u32[]{:S(2)}) collective-permute-start(bf16[3,3,1,16,512]{4,3,2,1,0:T(8,128)(2,1)S(1)} %pad_maximum_fusion.1), channel_id=1, source_target_pairs={{0,1},{1,2},{2,3},{4,5},{5,6},{6,7},{8,9},{9,10},{10,11},{12,13},{... | collective-permute-start | bytes 442376 | tf_op jit(solution)/shard_map/ppermute | solution.py:24
  240.8 23.7 %collective-permute-start.30 = (f32[16,512]{1,0:T(8,128)S(1)}, f32[16,512]{1,0:T(8,128)S(1)}, u32[]{:S(2)}, u32[]{:S(2)}) collective-permute-start(f32[16,512]{1,0:T(8,128)S(1)} %copy.175), channel_id=1, source_target_pairs={{0,8},{8,16},{16,24},{1,9},{9,17},{17,25},{2,10},{10,18},{18,26},{... | collective-permute-start | bytes 98312 | tf_op jit(solution)/shard_map/ppermute | solution.py:16
  247.3 18.5 %collective-permute-start.35 = (f32[16,512]{1,0:T(8,128)S(1)}, f32[16,512]{1,0:T(8,128)S(1)}, u32[]{:S(2)}, u32[]{:S(2)}) collective-permute-start(f32[16,512]{1,0:T(8,128)S(1)} %copy.185), channel_id=1, source_target_pairs={{1,0},{2,1},{3,2},{5,4},{6,5},{7,6},{9,8},{10,9},{11,10},{13,12},{... | collective-permute-start | bytes 98312 | tf_op jit(solution)/shard_map/ppermute | solution.py:16
  250.5 15.3 %collective-permute-start.34 = (f32[16,512]{1,0:T(8,128)S(1)}, f32[16,512]{1,0:T(8,128)S(1)}, u32[]{:S(2)}, u32[]{:S(2)}) collective-permute-start(f32[16,512]{1,0:T(8,128)S(1)} %copy.183), channel_id=1, source_target_pairs={{0,1},{1,2},{2,3},{4,5},{5,6},{6,7},{8,9},{9,10},{10,11},{12,13},{... | collective-permute-start | bytes 98312 | tf_op jit(solution)/shard_map/ppermute | solution.py:16
  256.7 9.0 %collective-permute-start.33 = (f32[16,512]{1,0:T(8,128)S(1)}, f32[16,512]{1,0:T(8,128)S(1)}, u32[]{:S(2)}, u32[]{:S(2)}) collective-permute-start(f32[16,512]{1,0:T(8,128)S(1)} %copy.181), channel_id=1, source_target_pairs={{4,0},{5,1},{6,2},{7,3},{12,8},{13,9},{14,10},{15,11},{20,16},{21,... | collective-permute-start | bytes 98312 | tf_op jit(solution)/shard_map/ppermute | solution.py:16
  259.7 6.1 %collective-permute-start.32 = (f32[16,512]{1,0:T(8,128)S(1)}, f32[16,512]{1,0:T(8,128)S(1)}, u32[]{:S(2)}, u32[]{:S(2)}) collective-permute-start(f32[16,512]{1,0:T(8,128)S(1)} %copy.179), channel_id=1, source_target_pairs={{0,4},{1,5},{2,6},{3,7},{8,12},{9,13},{10,14},{11,15},{16,20},{17,... | collective-permute-start | bytes 98312 | tf_op jit(solution)/shard_map/ppermute | solution.py:16
  264.5 7.0 %collective-permute-start.31 = (f32[16,512]{1,0:T(8,128)S(1)}, f32[16,512]{1,0:T(8,128)S(1)}, u32[]{:S(2)}, u32[]{:S(2)}) collective-permute-start(f32[16,512]{1,0:T(8,128)S(1)} %copy.177), channel_id=1, source_target_pairs={{8,0},{16,8},{24,16},{9,1},{17,9},{25,17},{10,2},{18,10},{26,18},{... | collective-permute-start | bytes 98312 | tf_op jit(solution)/shard_map/ppermute | solution.py:16
  314.5 23.1 %collective-permute-start.36 = (f32[16,512]{1,0:T(8,128)S(1)}, f32[16,512]{1,0:T(8,128)S(1)}, u32[]{:S(2)}, u32[]{:S(2)}) collective-permute-start(f32[16,512]{1,0:T(8,128)S(1)} %copy.187), channel_id=1, source_target_pairs={{0,8},{8,16},{16,24},{1,9},{9,17},{17,25},{2,10},{10,18},{18,26},{... | collective-permute-start | bytes 98312 | tf_op jit(solution)/shard_map/ppermute | solution.py:16
  320.3 18.5 %collective-permute-start.41 = (f32[16,512]{1,0:T(8,128)S(1)}, f32[16,512]{1,0:T(8,128)S(1)}, u32[]{:S(2)}, u32[]{:S(2)}) collective-permute-start(f32[16,512]{1,0:T(8,128)S(1)} %copy.197), channel_id=1, source_target_pairs={{1,0},{2,1},{3,2},{5,4},{6,5},{7,6},{9,8},{10,9},{11,10},{13,12},{... | collective-permute-start | bytes 98312 | tf_op jit(solution)/shard_map/ppermute | solution.py:16
  323.3 15.5 %collective-permute-start.40 = (f32[16,512]{1,0:T(8,128)S(1)}, f32[16,512]{1,0:T(8,128)S(1)}, u32[]{:S(2)}, u32[]{:S(2)}) collective-permute-start(f32[16,512]{1,0:T(8,128)S(1)} %copy.195), channel_id=1, source_target_pairs={{0,1},{1,2},{2,3},{4,5},{5,6},{6,7},{8,9},{9,10},{10,11},{12,13},{... | collective-permute-start | bytes 98312 | tf_op jit(solution)/shard_map/ppermute | solution.py:16
  329.6 9.3 %collective-permute-start.39 = (f32[16,512]{1,0:T(8,128)S(1)}, f32[16,512]{1,0:T(8,128)S(1)}, u32[]{:S(2)}, u32[]{:S(2)}) collective-permute-start(f32[16,512]{1,0:T(8,128)S(1)} %copy.193), channel_id=1, source_target_pairs={{4,0},{5,1},{6,2},{7,3},{12,8},{13,9},{14,10},{15,11},{20,16},{21,... | collective-permute-start | bytes 98312 | tf_op jit(solution)/shard_map/ppermute | solution.py:16
  332.6 6.3 %collective-permute-start.38 = (f32[16,512]{1,0:T(8,128)S(1)}, f32[16,512]{1,0:T(8,128)S(1)}, u32[]{:S(2)}, u32[]{:S(2)}) collective-permute-start(f32[16,512]{1,0:T(8,128)S(1)} %copy.191), channel_id=1, source_target_pairs={{0,4},{1,5},{2,6},{3,7},{8,12},{9,13},{10,14},{11,15},{16,20},{17,... | collective-permute-start | bytes 98312 | tf_op jit(solution)/shard_map/ppermute | solution.py:16
  343.4 6.2 %collective-permute-start.43 = (bf16[1,1,1,16,512]{4,3,2,1,0:T(8,128)(2,1)S(1)}, bf16[1,1,1,16,512]{4,3,2,1,0:T(8,128)(2,1)S(1)}, u32[]{:S(2)}, u32[]{:S(2)}) collective-permute-start(bf16[1,1,1,16,512]{4,3,2,1,0:T(8,128)(2,1)S(1)} %get-tuple-element.38), channel_id=1, source_target_pairs={{8,0},{16,8},{24,16},{9,1},{17,9},{25,17},{10,2},{18,10},{26,18},{... | collective-permute-start | bytes 49160 | tf_op jit(solution)/shard_map/ppermute | solution.py:27
  344.7 6.3 %collective-permute-start.42 = (bf16[1,1,1,16,512]{4,3,2,1,0:T(8,128)(2,1)S(1)}, bf16[1,1,1,16,512]{4,3,2,1,0:T(8,128)(2,1)S(1)}, u32[]{:S(2)}, u32[]{:S(2)}) collective-permute-start(bf16[1,1,1,16,512]{4,3,2,1,0:T(8,128)(2,1)S(1)} %get-tuple-element.38), channel_id=1, source_target_pairs={{0,8},{8,16},{16,24},{1,9},{9,17},{17,25},{2,10},{10,18},{18,26},{... | collective-permute-start | bytes 49160 | tf_op jit(solution)/shard_map/ppermute | solution.py:24
  351.0 6.5 %collective-permute-start.45 = (bf16[3,1,1,16,512]{4,3,2,1,0:T(8,128)(2,1)S(1)}, bf16[3,1,1,16,512]{4,3,2,1,0:T(8,128)(2,1)S(1)}, u32[]{:S(2)}, u32[]{:S(2)}) collective-permute-start(bf16[3,1,1,16,512]{4,3,2,1,0:T(8,128)(2,1)S(1)} %pad_maximum_fusion.5), channel_id=1, source_target_pairs={{4,0},{5,1},{6,2},{7,3},{12,8},{13,9},{14,10},{15,11},{20,16},{21,... | collective-permute-start | bytes 147464 | tf_op jit(solution)/shard_map/ppermute | solution.py:27
  357.5 8.0 %collective-permute-start.47 = (bf16[3,3,1,16,512]{4,3,2,1,0:T(8,128)(2,1)S(1)}, bf16[3,3,1,16,512]{4,3,2,1,0:T(8,128)(2,1)S(1)}, u32[]{:S(2)}, u32[]{:S(2)}) collective-permute-start(bf16[3,3,1,16,512]{4,3,2,1,0:T(8,128)(2,1)S(1)} %pad_maximum_fusion.2), channel_id=1, source_target_pairs={{1,0},{2,1},{3,2},{5,4},{6,5},{7,6},{9,8},{10,9},{11,10},{13,12},{... | collective-permute-start | bytes 442376 | tf_op jit(solution)/shard_map/ppermute | solution.py:27
  358.8 7.8 %collective-permute-start.46 = (bf16[3,3,1,16,512]{4,3,2,1,0:T(8,128)(2,1)S(1)}, bf16[3,3,1,16,512]{4,3,2,1,0:T(8,128)(2,1)S(1)}, u32[]{:S(2)}, u32[]{:S(2)}) collective-permute-start(bf16[3,3,1,16,512]{4,3,2,1,0:T(8,128)(2,1)S(1)} %pad_maximum_fusion.2), channel_id=1, source_target_pairs={{0,1},{1,2},{2,3},{4,5},{5,6},{6,7},{8,9},{9,10},{10,11},{12,13},{... | collective-permute-start | bytes 442376 | tf_op jit(solution)/shard_map/ppermute | solution.py:24
  374.1 23.5 %collective-permute-start.48 = (f32[16,512]{1,0:T(8,128)S(1)}, f32[16,512]{1,0:T(8,128)S(1)}, u32[]{:S(2)}, u32[]{:S(2)}) collective-permute-start(f32[16,512]{1,0:T(8,128)S(1)} %copy.211), channel_id=1, source_target_pairs={{0,8},{8,16},{16,24},{1,9},{9,17},{17,25},{2,10},{10,18},{18,26},{... | collective-permute-start | bytes 98312 | tf_op jit(solution)/shard_map/ppermute | solution.py:16
  380.6 18.3 %collective-permute-start.53 = (f32[16,512]{1,0:T(8,128)S(1)}, f32[16,512]{1,0:T(8,128)S(1)}, u32[]{:S(2)}, u32[]{:S(2)}) collective-permute-start(f32[16,512]{1,0:T(8,128)S(1)} %copy.221), channel_id=1, source_target_pairs={{1,0},{2,1},{3,2},{5,4},{6,5},{7,6},{9,8},{10,9},{11,10},{13,12},{... | collective-permute-start | bytes 98312 | tf_op jit(solution)/shard_map/ppermute | solution.py:16
  383.6 15.3 %collective-permute-start.52 = (f32[16,512]{1,0:T(8,128)S(1)}, f32[16,512]{1,0:T(8,128)S(1)}, u32[]{:S(2)}, u32[]{:S(2)}) collective-permute-start(f32[16,512]{1,0:T(8,128)S(1)} %copy.219), channel_id=1, source_target_pairs={{0,1},{1,2},{2,3},{4,5},{5,6},{6,7},{8,9},{9,10},{10,11},{12,13},{... | collective-permute-start | bytes 98312 | tf_op jit(solution)/shard_map/ppermute | solution.py:16
  389.8 9.0 %collective-permute-start.51 = (f32[16,512]{1,0:T(8,128)S(1)}, f32[16,512]{1,0:T(8,128)S(1)}, u32[]{:S(2)}, u32[]{:S(2)}) collective-permute-start(f32[16,512]{1,0:T(8,128)S(1)} %copy.217), channel_id=1, source_target_pairs={{4,0},{5,1},{6,2},{7,3},{12,8},{13,9},{14,10},{15,11},{20,16},{21,... | collective-permute-start | bytes 98312 | tf_op jit(solution)/shard_map/ppermute | solution.py:16
  392.8 6.1 %collective-permute-start.50 = (f32[16,512]{1,0:T(8,128)S(1)}, f32[16,512]{1,0:T(8,128)S(1)}, u32[]{:S(2)}, u32[]{:S(2)}) collective-permute-start(f32[16,512]{1,0:T(8,128)S(1)} %copy.215), channel_id=1, source_target_pairs={{0,4},{1,5},{2,6},{3,7},{8,12},{9,13},{10,14},{11,15},{16,20},{17,... | collective-permute-start | bytes 98312 | tf_op jit(solution)/shard_map/ppermute | solution.py:16
  397.5 7.0 %collective-permute-start.49 = (f32[16,512]{1,0:T(8,128)S(1)}, f32[16,512]{1,0:T(8,128)S(1)}, u32[]{:S(2)}, u32[]{:S(2)}) collective-permute-start(f32[16,512]{1,0:T(8,128)S(1)} %copy.213), channel_id=1, source_target_pairs={{8,0},{16,8},{24,16},{9,1},{17,9},{25,17},{10,2},{18,10},{26,18},{... | collective-permute-start | bytes 98312 | tf_op jit(solution)/shard_map/ppermute | solution.py:16
  (8 other events, 113.6 us)
where the time goes:
time: 456 us; the launch traced here: 447 us
  blocking collectives  163 us (36%)
  starting transfers between devices  146 us (32%)
  other arithmetic  58.2 us (13%)
  waiting for transfers between devices  34.7 us (8%)
  local copies, waits for them, and re-layouts  26.8 us (6%)
  matrix products  15.7 us (3%)
    psum x3, blocking collectives, local(): lax.psum((local_coeffs, inner_local(applied, applied), local_gram), ('gx'...  121 us
    ppermute x36, starting transfers between devices, from_behind(): return lax.ppermute(array, axis, pairs)  96.1 us
    scatter-add x36, other arithmetic, assemble(): jnp.zeros_like(result).at[:, owned_maps[facing]].add(face_blocks[facing])  53.8 us
    psum x1, blocking collectives, local(): initial = lax.psum(inner_local(target, target), ('gx', 'gy', 'gz'))  42 us
    ppermute x9, starting transfers between devices, with_halo(): lax.ppermute(lax.slice_in_dim(block, block.shape[dim] - width, None, axis...  37.9 us
    ppermute x36, waiting for transfers between devices, from_behind(): return lax.ppermute(array, axis, pairs)  30.4 us
    gather x36, local copies, waits for them, and re-layouts, gather_local(): jnp.take(ghost_layer[FACE_SPOTS[facing]], owned_maps[facing], axis=1)  16.6 us
    dot_general x3, matrix products, local(): jnp.dot(intersected, schur_block, preferred_element_type=jnp.float32)  13.7 us
  transfers between devices with their start and end apart: 54, of which 9 were waited for; matrix products, arithmetic and copies ran while one was open for 15% of the time, Pallas kernels for 0%

commit v1 on v0

v1 whole, which is shorter than its diff:
```python
import functools

import jax
import jax.numpy as jnp
from jax import lax
from jax.experimental import pallas as pl
from jax.experimental.pallas import tpu as pltpu
from jax.sharding import PartitionSpec as P

ITERS = 3
EPSILON = 1e-06
FACE_ORDER = (0, 1, 4, 5, 2, 3)
MESH = pl.DeviceIdType.MESH
BF16 = jnp.bfloat16
F32 = jnp.float32


def split(x):
    high = x.astype(BF16)
    low = (x - high.astype(F32)).astype(BF16)
    return jnp.concatenate([high, low], axis=0)


def merge(x):
    rows = x.shape[0] // 2
    return x[:rows] + x[rows:]


def mm(a, b):
    return jnp.dot(a, b, preferred_element_type=F32)


def rotate_solve(columns, beta_norm):
    num_cols = len(columns)
    rhs_vec = [beta_norm] + [jnp.zeros_like(beta_norm) for unused in range(num_cols)]
    cosines = []
    sines = []
    triangle = []
    for section in range(num_cols):
        column = [columns[section][row_at] for row_at in range(section + 2)]
        for earlier in range(section):
            rotated_a = cosines[earlier] * column[earlier] + sines[earlier] * column[earlier + 1]
            rotated_b = -sines[earlier] * column[earlier] + cosines[earlier] * column[earlier + 1]
            column[earlier] = rotated_a
            column[earlier + 1] = rotated_b
        radius = jnp.sqrt(
            column[section] * column[section] + column[section + 1] * column[section + 1]
        )
        cosine = column[section] / radius
        sine_val = column[section + 1] / radius
        column[section] = radius
        cosines.append(cosine)
        sines.append(sine_val)
        rhs_vec[section + 1] = -sine_val * rhs_vec[section]
        rhs_vec[section] = cosine * rhs_vec[section]
        triangle.append(column[: section + 1])
    coeffs = [None] * num_cols
    for section in reversed(range(num_cols)):
        running = rhs_vec[section]
        for onward in range(section + 1, num_cols):
            running = running - triangle[onward][section] * coeffs[onward]
        coeffs[section] = running / triangle[section][section]
    return (coeffs, jnp.abs(rhs_vec[num_cols]))


def kernel(
    sizes, g_ref, maps_ref, k_hbm, b_hbm, out_ref, ratio_ref,
    k_ref, b_ref, near_maps, gather_ref, scatter_ref, send_buf, recv_buf, acc_ref,
    t_ref, v_ref, z_ref, w_ref, last_ref, total_ref, plane_buf, line_buf,
    weight_sem, map_send, map_recv, send_sem, recv_sem,
    plane_send, plane_recv, line_send, line_recv,
):
    nx, ny, nz = sizes
    rhs, own = g_ref.shape
    face = maps_ref.shape[1]
    ix, iy, iz = lax.axis_index("gx"), lax.axis_index("gy"), lax.axis_index("gz")
    spots = ((ix, nx), (ix, nx), (iy, ny), (iy, ny), (iz, nz), (iz, nz))
    exists = [
        spots[f][0] > 0 if f % 2 == 0 else spots[f][0] < spots[f][1] - 1 for f in range(6)
    ]

    def across(f):
        step = 2 * (f % 2) - 1
        place = [ix, iy, iz]
        place[f // 2] = place[f // 2] + step
        return tuple(place)

    faces = [f for f in FACE_ORDER if spots[f][1] > 1]
    plane = [
        (lax.rem(ix + dx, nx), lax.rem(iy + dy, ny))
        for dx in range(nx) for dy in range(ny) if dx or dy
    ]
    line = [lax.rem(iz + dz, nz) for dz in range(1, nz)]

    weights = [pltpu.make_async_copy(b_hbm, b_ref, weight_sem.at[0])]
    weights.append(
        pltpu.make_async_copy(k_hbm.at[pl.ds(0, own)], k_ref.at[pl.ds(0, own)], weight_sem.at[1])
    )
    ghosts = pl.ds(own, k_ref.shape[0] - own)
    weights.append(pltpu.make_async_copy(k_hbm.at[ghosts], k_ref.at[ghosts], weight_sem.at[2]))
    for copy in weights:
        copy.start()

    barrier = pltpu.get_barrier_semaphore()
    for px, py in plane:
        pl.semaphore_signal(barrier, inc=1, device_id=(px, py, iz), device_id_type=MESH)
    for pz in line:
        pl.semaphore_signal(barrier, inc=1, device_id=(ix, iy, pz), device_id_type=MESH)

    t_ref[...] = g_ref[...]
    v_ref[...] = jnp.zeros_like(v_ref)
    z_ref[...] = jnp.zeros_like(z_ref)
    w_ref[...] = jnp.zeros_like(w_ref)
    last_ref[...] = jnp.zeros_like(last_ref)
    total_ref[...] = jnp.zeros_like(total_ref)
    for f in range(6):
        @pl.when(jnp.logical_not(exists[f]))
        def _():
            near_maps[f] = jnp.full(near_maps.shape[1:], -1, jnp.int32)
            for e in range(3 * ITERS):
                recv_buf[e, f] = jnp.zeros(recv_buf.shape[2:], BF16)

    pl.semaphore_wait(barrier, len(plane) + len(line))

    def map_copy(f, slot):
        return pltpu.make_async_remote_copy(
            src_ref=maps_ref, dst_ref=near_maps.at[slot], send_sem=map_send.at[f],
            recv_sem=map_recv.at[slot], device_id=across(f), device_id_type=MESH,
        )

    def face_copy(e, f, slot):
        return pltpu.make_async_remote_copy(
            src_ref=send_buf.at[e, f], dst_ref=recv_buf.at[e, slot], send_sem=send_sem.at[e, f],
            recv_sem=recv_sem.at[e, slot], device_id=across(f), device_id_type=MESH,
        )

    def plane_copy(r, peer, slot):
        mine = ix * ny + iy
        return pltpu.make_async_remote_copy(
            src_ref=plane_buf.at[r, mine], dst_ref=plane_buf.at[r, slot],
            send_sem=plane_send.at[r, peer[0] * ny + peer[1]], recv_sem=plane_recv.at[r, slot],
            device_id=(peer[0], peer[1], iz), device_id_type=MESH,
        )

    def line_copy(r, peer, slot):
        return pltpu.make_async_remote_copy(
            src_ref=line_buf.at[r, iz], dst_ref=line_buf.at[r, slot],
            send_sem=line_send.at[r, peer], recv_sem=line_recv.at[r, slot],
            device_id=(ix, iy, peer), device_id_type=MESH,
        )

    for f in faces:
        @pl.when(exists[f])
        def _():
            map_copy(f, f ^ 1).start()

    lanes = lax.broadcasted_iota(jnp.int32, (rhs, 128), 1)
    half = rhs // 2

    def start_sums(r):
        t = t_ref[...]
        last = last_ref[...]
        packed = jnp.where(lanes == ITERS, jnp.sum(t * t, axis=1, keepdims=True), 0.0)
        for k in range(ITERS):
            v = v_ref[k]
            packed = jnp.where(lanes == k, jnp.sum(v * t, axis=1, keepdims=True), packed)
            packed = jnp.where(
                lanes == ITERS + 1 + k, jnp.sum(v * last, axis=1, keepdims=True), packed
            )
        plane_buf[r, ix * ny + iy] = packed[:half] + pltpu.roll(packed[half:], 64, 1)
        for peer in plane:
            plane_copy(r, peer, ix * ny + iy).start()

    def pass_sums(r):
        for peer in plane:
            plane_copy(r, peer, peer[0] * ny + peer[1]).wait_recv()
        partial = plane_buf[r, 0]
        for at in range(1, nx * ny):
            partial = partial + plane_buf[r, at]
        line_buf[r, iz] = partial
        for peer in line:
            line_copy(r, peer, iz).start()

    def finish_sums(r):
        for peer in line:
            line_copy(r, peer, peer).wait_recv()
        total = line_buf[r, 0]
        for at in range(1, nz):
            total = total + line_buf[r, at]
        total_ref[r] = jnp.concatenate([total, pltpu.roll(total, 64, 1)], axis=0)

    def pick(r, lane):
        return jnp.sum(jnp.where(lanes == lane, total_ref[r], 0.0), axis=1, keepdims=True)

    def heights(r, count):
        coeffs = [pick(r, k) for k in range(count)]
        running = pick(r, ITERS)
        for k in range(count):
            running = running - 2.0 * coeffs[k] * coeffs[k]
            for n in range(k + 1):
                element = coeffs[k] * pick(k + 1, ITERS + 1 + n) * coeffs[n]
                running = running + (element if n == k else 2.0 * element)
        return coeffs, jnp.sqrt(jnp.maximum(running, 0.0) + EPSILON)

    def block(f):
        return pl.ds(own + f * face, face)

    def scattered(e, base):
        for f in faces:
            @pl.when(exists[f])
            def _():
                face_copy(e, f, f).wait_recv()
        added = mm(recv_buf[e, faces[0]], scatter_ref[faces[0]])
        for f in faces[1:]:
            added = added + mm(recv_buf[e, f], scatter_ref[f])
        return base + merge(added)

    def send(e, f, pair):
        send_buf[e, f] = pair

        @pl.when(exists[f])
        def _():
            face_copy(e, f, f ^ 1).start()

    def iteration(j, carry):
        first, second, third = 3 * j, 3 * j + 1, 3 * j + 2
        pair = split(t_ref[...])

        @pl.when(j == 0)
        def _():
            weights[0].wait()

        for f in faces:
            send(first, f, split(merge(mm(pair, b_ref[:, block(f)]))))
        start_sums(j)
        base = merge(mm(pair, b_ref[:, pl.ds(0, own)]))

        @pl.when(j == 0)
        def _():
            for f in faces:
                @pl.when(exists[f])
                def _():
                    map_copy(f, f).wait_recv()
            for f in faces:
                row = near_maps[f, pl.ds(f ^ 1, 1), :]
                hot = lax.broadcasted_iota(jnp.int32, (own, face), 0) == row
                hot = jnp.where(hot, 1.0, 0.0)
                gather_ref[f] = hot.astype(BF16)
                scatter_ref[f] = jnp.transpose(hot).astype(BF16)

        prepared = scattered(first, base)
        pair = split(prepared)
        for f in faces:
            send(second, f, mm(pair, gather_ref[f]).astype(BF16))
        pass_sums(j)

        @pl.when(j == 0)
        def _():
            weights[1].wait()

        acc_ref[...] = mm(pair, k_ref[pl.ds(0, own), :])

        @pl.when(j == 0)
        def _():
            weights[2].wait()

        for f in faces:
            @pl.when(exists[f])
            def _():
                face_copy(second, f, f).wait_recv()
        left = jnp.concatenate([recv_buf[second, f] for f in range(6)], axis=1)
        for f in faces:
            product = acc_ref[:, block(f)] + mm(left, k_ref[ghosts, block(f)])
            send(third, f, split(merge(product)))
        base = merge(acc_ref[:, pl.ds(0, own)] + mm(left, k_ref[ghosts, pl.ds(0, own)]))
        finish_sums(j)
        coeffs, height = heights(j, ITERS - 1)
        inverse = 1.0 / height
        newest = t_ref[...]
        for k in range(ITERS - 1):
            prepared = prepared - coeffs[k] * z_ref[k]
            newest = newest - coeffs[k] * v_ref[k]
        z_ref[j] = prepared * inverse
        newest = newest * inverse
        v_ref[j] = newest
        last_ref[...] = newest
        applied = scattered(third, base)
        for k in range(ITERS - 1):
            applied = applied - coeffs[k] * w_ref[k]
        applied = applied * inverse
        w_ref[j] = applied
        t_ref[...] = applied
        return carry

    lax.fori_loop(0, ITERS, iteration, 0)
    start_sums(ITERS)
    pass_sums(ITERS)
    finish_sums(ITERS)
    beta_norm = heights(0, 0)[1]
    columns = []
    for section in range(ITERS):
        coeffs, height = heights(section + 1, section + 1)
        columns.append(coeffs + [height])
    solved, remainder = rotate_solve(columns, beta_norm)
    adjoint = solved[0] * z_ref[0]
    for k in range(1, ITERS):
        adjoint = adjoint + solved[k] * z_ref[k]
    out_ref[...] = adjoint
    rows = lax.broadcasted_iota(jnp.int32, (rhs, 128), 0)
    spread = jnp.where(rows == lanes, remainder / beta_norm, 0.0)
    ratio_ref[...] = jnp.sum(spread, axis=0, keepdims=True)[:, :rhs]

    for f in faces:
        @pl.when(exists[f])
        def _():
            map_copy(f, f ^ 1).wait_send()
            for e in range(3 * ITERS):
                face_copy(e, f, f ^ 1).wait_send()
    for r in range(ITERS + 1):
        for peer in plane:
            plane_copy(r, peer, ix * ny + iy).wait_send()
        for peer in line:
            line_copy(r, peer, iz).wait_send()


def local(sizes, gradient, local_schur, inverse_rows, face_maps):
    nx, ny, nz = sizes
    target = gradient[0, 0, 0]
    rhs, own = target.shape
    maps = face_maps[0, 0, 0]
    face = maps.shape[1]
    whole = local_schur.shape[-1]
    exchanges = 3 * ITERS
    sums = ITERS + 1
    vmem = pl.BlockSpec(memory_space=pltpu.VMEM)
    hbm = pl.BlockSpec(memory_space=pl.ANY)
    dma = pltpu.SemaphoreType.DMA
    adjoint, ratio = pl.pallas_call(
        functools.partial(kernel, sizes),
        out_shape=(
            jax.ShapeDtypeStruct((rhs, own), F32),
            jax.ShapeDtypeStruct((1, rhs), F32),
        ),
        in_specs=[vmem, vmem, hbm, hbm],
        out_specs=(vmem, vmem),
        scratch_shapes=[
            pltpu.VMEM((whole, whole), BF16),
            pltpu.VMEM((own, whole), BF16),
            pltpu.VMEM((6,) + maps.shape, jnp.int32),
            pltpu.VMEM((6, own, face), BF16),
            pltpu.VMEM((6, face, own), BF16),
            pltpu.VMEM((exchanges, 6, 2 * rhs, face), BF16),
            pltpu.VMEM((exchanges, 6, 2 * rhs, face), BF16),
            pltpu.VMEM((2 * rhs, whole), F32),
            pltpu.VMEM((rhs, own), F32),
            pltpu.VMEM((ITERS, rhs, own), F32),
            pltpu.VMEM((ITERS, rhs, own), F32),
            pltpu.VMEM((ITERS, rhs, own), F32),
            pltpu.VMEM((rhs, own), F32),
            pltpu.VMEM((sums, rhs, 128), F32),
            pltpu.VMEM((sums, nx * ny, rhs // 2, 128), F32),
            pltpu.VMEM((sums, nz, rhs // 2, 128), F32),
            dma((3,)),
            dma((6,)),
            dma((6,)),
            dma((exchanges, 6)),
            dma((exchanges, 6)),
            dma((sums, nx * ny)),
            dma((sums, nx * ny)),
            dma((sums, nz)),
            dma((sums, nz)),
        ],
        compiler_params=pltpu.CompilerParams(
            collective_id=0, has_side_effects=True, vmem_limit_bytes=56 * 1024 * 1024
        ),
    )(target, maps, local_schur[0, 0, 0], inverse_rows[0, 0, 0])
    return (adjoint[None, None, None], ratio[0])


def solution(mesh):
    placed = P("gx", "gy", "gz", None, None)
    sizes = (mesh.shape["gx"], mesh.shape["gy"], mesh.shape["gz"])
    return jax.shard_map(
        functools.partial(local, sizes),
        mesh=mesh,
        in_specs=(placed, placed, placed, placed),
        out_specs=(placed, P()),
        check_vma=False,
    )
```

time: 456 us -> 55.9 us (0.12); the launches traced: 447 us -> 55.6 us
  blocking collectives: 163 us -> 0 us
  starting transfers between devices: 146 us -> 0 us
  other arithmetic: 58.2 us -> 0 us
  Pallas kernels: 0 us -> 51.1 us
  waiting for transfers between devices: 34.7 us -> 0 us
  local copies, waits for them, and re-layouts: 26.8 us -> 3.84 us
  matrix products: 15.7 us -> 0 us
    psum x4 -> x0, blocking collectives: 163 us -> none  [the longest x3 121 us: local(): lax.psum((local_coeffs, inner_local(applied, applied), local_gram), ('gx'...]
    ppermute x54 -> x0, starting transfers between devices: 146 us -> none  [the longest x36 96.1 us: from_behind(): return lax.ppermute(array, axis, pairs)]
    scatter-add x36 -> x0, other arithmetic: 53.8 us -> none  [assemble(): jnp.zeros_like(result).at[:, owned_maps[facing]].add(face_blocks[facing])]
    pallas_call x0 -> x1, Pallas kernels: none -> 51.1 us  [local(): pl.pallas_call(functools.partial(kernel, sizes), out_shape=(jax.ShapeDtyp...]
    ppermute x54 -> x0, waiting for transfers between devices: 34.7 us -> none  [the longest x36 30.4 us: from_behind(): return lax.ppermute(array, axis, pairs)]
    gather x36 -> x0, local copies, waits for them, and re-layouts: 16.6 us -> none  [gather_local(): jnp.take(ghost_layer[FACE_SPOTS[facing]], owned_maps[facing], axis=1)]
    dot_general x6 -> x0, matrix products: 15.7 us -> none  [the longest x3 13.7 us: local(): jnp.dot(intersected, schur_block, preferred_element_type=jnp.float32)]
  transfers between devices with their start and end apart: 54 -> 0, of which waited for: 9 -> 0; matrix products, arithmetic and copies ran while one was open for 15% -> 0% of each run, Pallas kernels for 0% -> 0%
where the time goes in v1:
time: 55.9 us; the launch traced here: 55.6 us
  Pallas kernels  51.1 us (91%)
  local copies, waits for them, and re-layouts  3.84 us (7%)
  between operations  0.64 us (1%)
    pallas_call x1, Pallas kernels, local(): pl.pallas_call(functools.partial(kernel, sizes), out_shape=(jax.ShapeDtyp...  51.1 us
    unnamed x3, local copies, waits for them, and re-layouts  3.84 us

profile of v1, /device:TPU:0, one launch (start us, length us, event | category | flops | bytes accessed | tf_op | source)
XLA Modules:
  0.0 55.6 jit_solution(12209706088613769251)
XLA Ops:
  0.6 1.3 %copy.8 = s32[1,1,1,6,256]{4,3,2,1,0:T(8,128)} copy(s32[1,1,1,6,256]{4,2,3,1,0:T(1,128)} %param.7) | data formatting | bytes 12288
  1.9 51.1 %shard_map.59 = (f32[16,512]{1,0:T(8,128)}, f32[1,16]{1,0:T(1,128)}) custom-call(f32[16,512]{1,0:T(8,128)} %bitcast.10, s32[6,256]{1,0:T(8,128)} %bitcast.12, bf16[2048,2048]{1,0:T(8,128)(2,1)} %bitcast.8, bf16[512,2048]{1,0:T(8,128)(2,1)} %bitcast.9), custom_call_target="tpu_custom_call" | custom-call | tf_op jit(solution)/shard_map/pallas_call | solution.py:338
  53.0 1.4 %copy.11 = f32[1,1,1,16,512]{4,3,2,1,0:T(8,128)} copy(f32[1,1,1,16,512]{4,3,2,1,0:T(8,128)} %bitcast.11) | data formatting | bytes 65536
  54.4 1.2 %copy.12 = f32[16]{0:T(128)} copy(f32[16]{0:T(128)} %bitcast.13) | data formatting | bytes 128

commit v2 on v1

--- a/solution.py
+++ b/solution.py
@@ -9,7 +9,8 @@
 
 ITERS = 3
 EPSILON = 1e-06
-FACE_ORDER = (0, 1, 4, 5, 2, 3)
+FAR = (0, 1)
+NEAR = (4, 5, 2, 3)
 MESH = pl.DeviceIdType.MESH
 BF16 = jnp.bfloat16
 F32 = jnp.float32
@@ -66,13 +67,13 @@
 def kernel(
     sizes, g_ref, maps_ref, k_hbm, b_hbm, out_ref, ratio_ref,
     k_ref, b_ref, near_maps, gather_ref, scatter_ref, send_buf, recv_buf, acc_ref,
-    t_ref, v_ref, z_ref, w_ref, last_ref, total_ref, plane_buf, line_buf,
+    base_ref, t_ref, v_ref, z_ref, w_ref, last_ref, total_ref, plane_buf, line_buf,
     weight_sem, map_send, map_recv, send_sem, recv_sem,
     plane_send, plane_recv, line_send, line_recv,
 ):
     nx, ny, nz = sizes
     rhs, own = g_ref.shape
-    face = maps_ref.shape[1]
+    face = maps_ref.shape[-1]
     ix, iy, iz = lax.axis_index("gx"), lax.axis_index("gy"), lax.axis_index("gz")
     spots = ((ix, nx), (ix, nx), (iy, ny), (iy, ny), (iz, nz), (iz, nz))
     exists = [
@@ -85,7 +86,10 @@
         place[f // 2] = place[f // 2] + step
         return tuple(place)
 
-    faces = [f for f in FACE_ORDER if spots[f][1] > 1]
+    faces = [f for f in FAR + NEAR if spots[f][1] > 1]
+    far_width, near_width = len(FAR) * face, len(NEAR) * face
+    far_columns = pl.ds(own, far_width)
+    near_columns = pl.ds(own + far_width, near_width)
     plane = [
         (lax.rem(ix + dx, nx), lax.rem(iy + dy, ny))
         for dx in range(nx) for dy in range(ny) if dx or dy
@@ -120,8 +124,6 @@
             for e in range(3 * ITERS):
                 recv_buf[e, f] = jnp.zeros(recv_buf.shape[2:], BF16)
 
-    pl.semaphore_wait(barrier, len(plane) + len(line))
-
     def map_copy(f, slot):
         return pltpu.make_async_remote_copy(
             src_ref=maps_ref, dst_ref=near_maps.at[slot], send_sem=map_send.at[f],
@@ -149,25 +151,24 @@
             device_id=(ix, iy, peer), device_id_type=MESH,
         )
 
-    for f in faces:
-        @pl.when(exists[f])
-        def _():
-            map_copy(f, f ^ 1).start()
-
     lanes = lax.broadcasted_iota(jnp.int32, (rhs, 128), 1)
-    half = rhs // 2
+    rows = lax.broadcasted_iota(jnp.int32, (rhs, 128), 0)
+    group = 128 // rhs
+    places = lax.rem(lanes, group)
+    mine = lax.div(lanes, group) == rows
 
     def start_sums(r):
         t = t_ref[...]
         last = last_ref[...]
-        packed = jnp.where(lanes == ITERS, jnp.sum(t * t, axis=1, keepdims=True), 0.0)
+        packed = jnp.where(places == ITERS, jnp.sum(t * t, axis=1, keepdims=True), 0.0)
         for k in range(ITERS):
             v = v_ref[k]
-            packed = jnp.where(lanes == k, jnp.sum(v * t, axis=1, keepdims=True), packed)
+            packed = jnp.where(places == k, jnp.sum(v * t, axis=1, keepdims=True), packed)
             packed = jnp.where(
-                lanes == ITERS + 1 + k, jnp.sum(v * last, axis=1, keepdims=True), packed
+                places == ITERS + 1 + k, jnp.sum(v * last, axis=1, keepdims=True), packed
             )
-        plane_buf[r, ix * ny + iy] = packed[:half] + pltpu.roll(packed[half:], 64, 1)
+        packed = jnp.where(mine, packed, 0.0)
+        plane_buf[r, ix * ny + iy] = jnp.sum(packed, axis=0, keepdims=True)
         for peer in plane:
             plane_copy(r, peer, ix * ny + iy).start()
 
@@ -187,10 +188,10 @@
         total = line_buf[r, 0]
         for at in range(1, nz):
             total = total + line_buf[r, at]
-        total_ref[r] = jnp.concatenate([total, pltpu.roll(total, 64, 1)], axis=0)
+        total_ref[r] = jnp.where(mine, total, 0.0)
 
     def pick(r, lane):
-        return jnp.sum(jnp.where(lanes == lane, total_ref[r], 0.0), axis=1, keepdims=True)
+        return jnp.sum(jnp.where(places == lane, total_ref[r], 0.0), axis=1, keepdims=True)
 
     def heights(r, count):
         coeffs = [pick(r, k) for k in range(count)]
@@ -202,38 +203,52 @@
                 running = running + (element if n == k else 2.0 * element)
         return coeffs, jnp.sqrt(jnp.maximum(running, 0.0) + EPSILON)
 
-    def block(f):
-        return pl.ds(own + f * face, face)
+    def arrived(e, group):
+        for f in group:
+            if f in faces:
+                @pl.when(exists[f])
+                def _():
+                    face_copy(e, f, f).wait_recv()
+        return jnp.concatenate([recv_buf[e, f] for f in sorted(group)], axis=1)
 
     def scattered(e, base):
-        for f in faces:
-            @pl.when(exists[f])
-            def _():
-                face_copy(e, f, f).wait_recv()
-        added = mm(recv_buf[e, faces[0]], scatter_ref[faces[0]])
-        for f in faces[1:]:
-            added = added + mm(recv_buf[e, f], scatter_ref[f])
+        added = mm(arrived(e, NEAR), scatter_ref[pl.ds(far_width, near_width), :])
+        added = added + mm(arrived(e, FAR), scatter_ref[pl.ds(0, far_width), :])
         return base + merge(added)
 
-    def send(e, f, pair):
-        send_buf[e, f] = pair
-
-        @pl.when(exists[f])
-        def _():
-            face_copy(e, f, f ^ 1).start()
+    def stage(e, group, pairs):
+        for at, f in enumerate(sorted(group)):
+            send_buf[e, f] = pairs[:, at * face : (at + 1) * face]
+
+    def send(e, group):
+        odd = lax.rem(ix, 2) == 1
+
+        def start(f, when):
+            if f in faces:
+                @pl.when(jnp.logical_and(exists[f], when))
+                def _():
+                    face_copy(e, f, f ^ 1).start()
+
+        if group is FAR:
+            start(1, odd)
+            start(0, True)
+            start(1, jnp.logical_not(odd))
+        else:
+            for f in group:
+                start(f, True)
+
+    def precondition(e, ready):
+        pair = split(t_ref[...])
+        stage(e, FAR, split(merge(mm(pair, b_ref[:, far_columns]))))
+        ready()
+        send(e, FAR)
+        stage(e, NEAR, split(merge(mm(pair, b_ref[:, near_columns]))))
+        send(e, NEAR)
+        base_ref[...] = merge(mm(pair, b_ref[:, pl.ds(0, own)]))
 
     def iteration(j, carry):
         first, second, third = 3 * j, 3 * j + 1, 3 * j + 2
-        pair = split(t_ref[...])
-
-        @pl.when(j == 0)
-        def _():
-            weights[0].wait()
-
-        for f in faces:
-            send(first, f, split(merge(mm(pair, b_ref[:, block(f)]))))
         start_sums(j)
-        base = merge(mm(pair, b_ref[:, pl.ds(0, own)]))
 
         @pl.when(j == 0)
         def _():
@@ -241,17 +256,19 @@
                 @pl.when(exists[f])
                 def _():
                     map_copy(f, f).wait_recv()
-            for f in faces:
-                row = near_maps[f, pl.ds(f ^ 1, 1), :]
+            for f in range(6):
+                row = near_maps[f, f ^ 1]
                 hot = lax.broadcasted_iota(jnp.int32, (own, face), 0) == row
                 hot = jnp.where(hot, 1.0, 0.0)
-                gather_ref[f] = hot.astype(BF16)
-                scatter_ref[f] = jnp.transpose(hot).astype(BF16)
-
-        prepared = scattered(first, base)
+                gather_ref[:, pl.ds(f * face, face)] = hot.astype(BF16)
+                scatter_ref[pl.ds(f * face, face), :] = jnp.transpose(hot).astype(BF16)
+
+        prepared = scattered(first, base_ref[...])
         pair = split(prepared)
-        for f in faces:
-            send(second, f, mm(pair, gather_ref[f]).astype(BF16))
+        stage(second, FAR, mm(pair, gather_ref[:, pl.ds(0, far_width)]).astype(BF16))
+        send(second, FAR)
+        stage(second, NEAR, mm(pair, gather_ref[:, pl.ds(far_width, near_width)]).astype(BF16))
+        send(second, NEAR)
         pass_sums(j)
 
         @pl.when(j == 0)
@@ -264,15 +281,17 @@
         def _():
             weights[2].wait()
 
-        for f in faces:
-            @pl.when(exists[f])
-            def _():
-                face_copy(second, f, f).wait_recv()
-        left = jnp.concatenate([recv_buf[second, f] for f in range(6)], axis=1)
-        for f in faces:
-            product = acc_ref[:, block(f)] + mm(left, k_ref[ghosts, block(f)])
-            send(third, f, split(merge(product)))
-        base = merge(acc_ref[:, pl.ds(0, own)] + mm(left, k_ref[ghosts, pl.ds(0, own)]))
+        acc_ref[...] += mm(arrived(second, NEAR), k_ref[near_columns, :])
+        left = arrived(second, FAR)
+
+        def products(columns):
+            return merge(acc_ref[:, columns] + mm(left, k_ref[far_columns, columns]))
+
+        stage(third, FAR, split(products(far_columns)))
+        send(third, FAR)
+        stage(third, NEAR, split(products(near_columns)))
+        send(third, NEAR)
+        base = products(pl.ds(0, own))
         finish_sums(j)
         coeffs, height = heights(j, ITERS - 1)
         inverse = 1.0 / height
@@ -290,8 +309,23 @@
         applied = applied * inverse
         w_ref[j] = applied
         t_ref[...] = applied
+
+        @pl.when(j < ITERS - 1)
+        def _():
+            precondition(3 * j + 3, lambda: None)
+
         return carry
 
+
+    def ready():
+        pl.semaphore_wait(barrier, len(plane) + len(line))
+
+    weights[0].wait()
+    precondition(0, ready)
+    for f in faces:
+        @pl.when(exists[f])
+        def _():
+            map_copy(f, f ^ 1).start()
     lax.fori_loop(0, ITERS, iteration, 0)
     start_sums(ITERS)
     pass_sums(ITERS)
@@ -306,7 +340,6 @@
     for k in range(1, ITERS):
         adjoint = adjoint + solved[k] * z_ref[k]
     out_ref[...] = adjoint
-    rows = lax.broadcasted_iota(jnp.int32, (rhs, 128), 0)
     spread = jnp.where(rows == lanes, remainder / beta_norm, 0.0)
     ratio_ref[...] = jnp.sum(spread, axis=0, keepdims=True)[:, :rhs]
 
@@ -327,8 +360,8 @@
     nx, ny, nz = sizes
     target = gradient[0, 0, 0]
     rhs, own = target.shape
-    maps = face_maps[0, 0, 0]
-    face = maps.shape[1]
+    maps = jnp.swapaxes(face_maps[0, 0], 0, 1)
+    face = maps.shape[-1]
     whole = local_schur.shape[-1]
     exchanges = 3 * ITERS
     sums = ITERS + 1
@@ -338,8 +371,8 @@
     adjoint, ratio = pl.pallas_call(
         functools.partial(kernel, sizes),
         out_shape=(
-            jax.ShapeDtypeStruct((rhs, own), F32),
-            jax.ShapeDtypeStruct((1, rhs), F32),
+            pltpu.VMEM((rhs, own), F32),
+            pltpu.VMEM((1, rhs), F32),
         ),
         in_specs=[vmem, vmem, hbm, hbm],
         out_specs=(vmem, vmem),
@@ -347,19 +380,20 @@
             pltpu.VMEM((whole, whole), BF16),
             pltpu.VMEM((own, whole), BF16),
             pltpu.VMEM((6,) + maps.shape, jnp.int32),
-            pltpu.VMEM((6, own, face), BF16),
-            pltpu.VMEM((6, face, own), BF16),
+            pltpu.VMEM((own, 6 * face), BF16),
+            pltpu.VMEM((6 * face, own), BF16),
             pltpu.VMEM((exchanges, 6, 2 * rhs, face), BF16),
             pltpu.VMEM((exchanges, 6, 2 * rhs, face), BF16),
             pltpu.VMEM((2 * rhs, whole), F32),
+            pltpu.VMEM((rhs, own), F32),
             pltpu.VMEM((rhs, own), F32),
             pltpu.VMEM((ITERS, rhs, own), F32),
             pltpu.VMEM((ITERS, rhs, own), F32),
             pltpu.VMEM((ITERS, rhs, own), F32),
             pltpu.VMEM((rhs, own), F32),
             pltpu.VMEM((sums, rhs, 128), F32),
-            pltpu.VMEM((sums, nx * ny, rhs // 2, 128), F32),
-            pltpu.VMEM((sums, nz, rhs // 2, 128), F32),
+            pltpu.VMEM((sums, nx * ny, 1, 128), F32),
+            pltpu.VMEM((sums, nz, 1, 128), F32),
             dma((3,)),
             dma((6,)),
             dma((6,)),

time: 55.9 us -> 51.8 us (0.927)
  local copies, waits for them, and re-layouts: 3.84 us -> 1.13 us
  Pallas kernels: 51.1 us -> 49.8 us
    unnamed x3 -> x2, local copies, waits for them, and re-layouts: 3.84 us -> 1.13 us
    pallas_call x1, Pallas kernels: 51.1 us -> 49.8 us  [local(): pl.pallas_call(functools.partial(kernel, sizes), out_shape=(pltpu.VMEM((r...]
where the time goes in v2:
time: 51.8 us; the launch traced here: 51.6 us
  Pallas kernels  49.8 us (96%)
  local copies, waits for them, and re-layouts  1.13 us (2%)
  between operations  0.64 us (1%)
    pallas_call x1, Pallas kernels, local(): pl.pallas_call(functools.partial(kernel, sizes), out_shape=(pltpu.VMEM((r...  49.8 us
    unnamed x2, local copies, waits for them, and re-layouts  1.13 us

profile of v2, /device:TPU:0, one launch (start us, length us, event | category | flops | bytes accessed | tf_op | source)
XLA Modules:
  0.0 51.6 jit_solution(115103890857314983)
XLA Ops:
  0.6 49.8 %shard_map.59 = (f32[16,512]{1,0:T(8,128)S(1)}, f32[1,16]{1,0:T(1,128)S(1)}) custom-call(f32[16,512]{1,0:T(8,128)} %bitcast.10, s32[6,1,256]{2,1,0:T(1,128)} %bitcast.11, bf16[2048,2048]{1,0:T(8,128)(2,1)} %bitcast.8, bf16[512,2048]{1,0:T(8,128)(2,1)} %bitcast.9), custom_call_target="tpu_custom_call" | custom-call | tf_op jit(solution)/shard_map/pallas_call | solution.py:371
  50.5 0.6 %copy.8 = f32[1,1,1,16,512]{4,3,2,1,0:T(8,128)} copy(f32[1,1,1,16,512]{4,3,2,1,0:T(8,128)S(1)} %bitcast.6) | data formatting | bytes 65536
  51.1 0.5 copy.9
